TPU v7x, 32 devices: a whole 2x2x4 slice. The times are simulated.
32 devices in a mesh: tensor: 2 (over x), context: 8 (over z, core), dp: 2 (over y).
Axes of the slice: x: 2, y: 2, z: 4, core: 2. Of those that a mesh axis runs over, the one named last changes fastest.
Arguments:
- query_a: bfloat16 [2048, 1024], P(('dp', 'context'), 'tensor'), parts along dimension 0, may hold values from -5 to 5
- key_a: bfloat16 [2048, 256], P(('dp', 'context'), 'tensor'), parts along dimension 0, may hold values from -5 to 5
- value_a: bfloat16 [2048, 256], P(('dp', 'context'), 'tensor'), parts along dimension 0, may hold values from -12 to 12
- grad_out_a: bfloat16 [2048, 1024], P(('dp', 'context'), 'tensor'), parts along dimension 0, may hold values from -6 to 6
- query_b: bfloat16 [2048, 1024], P(('dp', 'context'), 'tensor'), parts along dimension 0, may hold values from -5 to 5
- key_b: bfloat16 [2048, 256], P(('dp', 'context'), 'tensor'), parts along dimension 0, may hold values from -5 to 5
- value_b: bfloat16 [2048, 256], P(('dp', 'context'), 'tensor'), parts along dimension 0, may hold values from -12 to 12
- slab_owner: int32 [8], replicated, may hold values from 0 to 7, each once
Outputs:
- out_b: bfloat16 [2048, 1024], P(('dp', 'context'), 'tensor'), parts along dimension 0
- grad_query_a: bfloat16 [2048, 1024], P(('dp', 'context'), 'tensor'), parts along dimension 0
- grad_key_a: bfloat16 [2048, 256], P(('dp', 'context'), 'tensor'), parts along dimension 0
- grad_value_a: bfloat16 [2048, 256], P(('dp', 'context'), 'tensor'), parts along dimension 0
There are 2 independent parts, one for each index of `dp`. A program takes and returns all parts, laid end to end along the dimension named above; an argument that names none is the same for every part. Nothing has to cross between parts.
Inputs may be any that keep to these rules, and one draw needn't show every extreme that they name: `slab_owner`: each number appears once.
All inputs are finite; a program needn't handle non-finite values.
Results may differ from a plain program's by a relative error of at most 0.0091.
Values may be sent and summed in bfloat16 or wider, within the bound.
A program may use at most 64 MiB of HBM per device.

v0:
```python
import functools

import jax
import jax.numpy as jnp
from jax import lax
from jax.experimental import pallas as pl
from jax.experimental.pallas import tpu as pltpu
from jax.sharding import PartitionSpec as P

LOW = -1e30
LOG2E = 1.4426950408889634
F32 = jnp.float32
BF16 = jnp.bfloat16


def dot_nt(a, b):
    return lax.dot_general(a, b, (((1,), (1,)), ((), ())), preferred_element_type=F32)


def dot_nn(a, b):
    return lax.dot_general(a, b, (((1,), (0,)), ((), ())), preferred_element_type=F32)


def dot_tn(a, b):
    return lax.dot_general(a, b, (((0,), (0,)), ((), ())), preferred_element_type=F32)


def groups(x, op):
    out = x[0:8]
    for i in range(8, x.shape[0], 8):
        out = op(out, x[i:i + 8])
    return out


def kernel(
    n, tok, heads, dim,
    owner, qa, ka, va, ga, qb, kb, vb,
    out_b, out_dq, out_dk, out_dv,
    kv, q_a, g_a, q_b, scores, pgrad, top, tot, dsum, acc_t, both,
    own, pair_out, pair_in, far_out, far_in,
    load_sem, recv_sem, right_sem, left_sem, mate_sem,
    pair_send, pair_recv, far_send, far_recv,
):
    chips = n // 2
    me = lax.axis_index("context")
    chip, core = me // 2, me % 2
    mate = chip * 2 + (1 - core)
    rows = heads * tok
    half = tok // 2
    scale = dim ** (-0.5)
    factor = scale * LOG2E

    def to(idx):
        return dict(device_id={"context": idx}, device_id_type=pl.DeviceIdType.MESH)

    def kv_load(b, j):
        src = ((ka, va), (kb, vb))[b][j]
        return pltpu.make_async_copy(src, kv.at[b, me, j], load_sem.at[b * 2 + j])

    def head_load(i, h):
        src, dst = ((qa, q_a), (ga, g_a), (qb, q_b))[i]
        return pltpu.make_async_copy(
            src.at[:, pl.ds(h * dim, dim)], dst.at[pl.ds(h * tok, tok), :],
            load_sem.at[4 + i * heads + h],
        )

    for b in range(2):
        for j in range(2):
            kv_load(b, j).start()
    for i in range(3):
        for h in range(heads):
            head_load(i, h).start()

    barrier = pltpu.get_barrier_semaphore()
    for off in range(1, chips):
        pl.semaphore_signal(barrier, inc=1, **to(lax.rem(chip + off, chips) * 2 + core))
    pl.semaphore_signal(barrier, inc=1, **to(mate))
    for b in range(2):
        for j in range(2):
            kv_load(b, j).wait()
    pl.semaphore_wait(barrier, chips)

    def hop(b, slot, j, target, sems):
        return pltpu.make_async_remote_copy(
            src_ref=kv.at[b, slot, j], dst_ref=kv.at[b, slot, j],
            send_sem=sems.at[b, slot, j], recv_sem=recv_sem.at[b, slot, j], **to(target),
        )

    def go_right(b, slot, j):
        return hop(b, slot, j, jnp.minimum(me + 2, n - 1), right_sem)

    def go_left(b, slot, j):
        return hop(b, slot, j, jnp.maximum(me - 2, 0), left_sem)

    def go_mate(b, slot, j):
        return hop(b, slot, j, mate, mate_sem)

    can_right = chip + 1 < chips
    can_left = chip > 0

    def spread_own(b):
        @pl.when(can_right)
        def _():
            for j in range(2):
                go_right(b, me, j).start()

        @pl.when(can_left)
        def _():
            for j in range(2):
                go_left(b, me, j).start()

        for j in range(2):
            go_mate(b, me, j).start()

    def relay(b, t):
        from_left = me - 2 * t
        from_right = me + 2 * t
        for j in range(2):
            @pl.when(chip - t >= 0)
            def _():
                slot = jnp.maximum(from_left, 0)
                hop(b, slot, j, mate, mate_sem).wait_recv()

                @pl.when(can_right)
                def _():
                    go_right(b, slot, j).start()
                go_mate(b, slot, j).start()

            @pl.when(chip + t < chips)
            def _():
                slot = jnp.minimum(from_right, n - 1)
                hop(b, slot, j, mate, mate_sem).wait_recv()

                @pl.when(can_left)
                def _():
                    go_left(b, slot, j).start()
                go_mate(b, slot, j).start()

    def take_mate(b, slot):
        for j in range(2):
            hop(b, slot, j, mate, mate_sem).wait_recv()

    spread_own(0)
    spread_own(1)

    lane = lax.broadcasted_iota(jnp.int32, (1, rows), 1) % tok
    mine = owner[me]
    places = jnp.where(lane < half, mine * half + lane, (2 * n - 1 - mine) * half + lane - half)
    key_row = lax.broadcasted_iota(jnp.int32, (half, rows), 0)

    def score_pair(b, d, queries):
        keys = kv[b, pl.ds(2 * d, 2), 0].reshape(2 * tok, dim)
        raw = dot_nt(keys, queries[...])
        best = top[...]
        for c in range(2):
            o = owner[2 * d + c]
            for part, slab in ((0, o), (1, 2 * n - 1 - o)):
                lo = c * tok + part * half
                piece = jnp.where(key_row <= places - slab * half, raw[lo:lo + half], LOW)
                scores[d, lo:lo + half] = piece
                best = jnp.maximum(best, groups(piece, jnp.maximum))
        top[...] = best

    def first_a(d):
        take_mate(0, 2 * d + 1 - core)
        score_pair(0, d, q_a)
        pgrad[d] = dot_nt(kv[0, pl.ds(2 * d, 2), 1].reshape(2 * tok, dim), g_a[...])

    for i in range(3):
        for h in range(heads):
            head_load(i, h).wait()
    top[...] = jnp.full_like(top, LOW)

    def gather_a(t, _):
        relay(0, t)

        @pl.when(chip - t + 1 >= 0)
        def _():
            first_a(jnp.maximum(chip - t + 1, 0))

        @pl.when(jnp.logical_and(chip + t - 1 < chips, t > 1))
        def _():
            first_a(jnp.minimum(chip + t - 1, chips - 1))

        @pl.when(t < chips - 1)
        def _():
            relay(1, t)
        return 0

    lax.fori_loop(1, chips, gather_a, 0)

    @pl.when(chip == chips - 1)
    def _():
        first_a(0)

    @pl.when(chip == 0)
    def _():
        first_a(chips - 1)

    relay(1, chips - 1)

    peak = jnp.max(top[...], axis=0, keepdims=True) * factor
    tot[...] = jnp.zeros_like(tot)
    dsum[...] = jnp.zeros_like(dsum)

    def second_a(i, _):
        p = jnp.exp2(scores[i] * factor - peak)
        scores[i] = p
        tot[...] += groups(p, jnp.add)
        dsum[...] += groups(p * pgrad[i], jnp.add)
        return 0

    lax.fori_loop(0, chips, second_a, 0)
    inv = 1.0 / jnp.sum(tot[...], axis=0, keepdims=True)
    delta = jnp.sum(dsum[...], axis=0, keepdims=True) * inv
    acc_t[...] = jnp.zeros_like(acc_t)

    def grads(d):
        prob = scores[d] * inv
        sg = (prob * (pgrad[d] - delta)).astype(BF16)
        both[0] = dot_nn(sg, q_a[...]).reshape(2, tok, dim)
        both[1] = dot_nn(prob.astype(BF16), g_a[...]).reshape(2, tok, dim)
        acc_t[...] += dot_tn(kv[0, pl.ds(2 * d, 2), 0].reshape(2 * tok, dim), sg)

    def pair(d):
        return pltpu.make_async_remote_copy(
            src_ref=pair_out.at[d], dst_ref=pair_in.at[d],
            send_sem=pair_send.at[d], recv_sem=pair_recv.at[d], **to(mate),
        )

    def far(d):
        return pltpu.make_async_remote_copy(
            src_ref=far_out.at[d], dst_ref=far_in.at[chip],
            send_sem=far_send.at[d], recv_sem=far_recv.at[chip], **to(d * 2 + core),
        )

    def ship(d):
        pair(d).wait_recv()
        far_out[d] = (own[d] + pair_in[d].astype(F32)).astype(BF16)
        far(d).start()

    def third_a(t, _):
        d = lax.rem(chip + t + 1, chips)
        grads(d)
        for j in range(2):
            pair_out[d, j] = both[j, 1 - core].astype(BF16)
        pair(d).start()
        for j in range(2):
            own[d, j] = both[j, core]

        @pl.when(t >= 1)
        def _():
            ship(lax.rem(chip + t, chips))
        return 0

    lax.fori_loop(0, chips, third_a, 0)

    def put(out, x):
        low = jnp.transpose(x).astype(BF16)
        for h in range(heads):
            out[:, h * dim:(h + 1) * dim] = low[h * tok:(h + 1) * tok]

    put(out_dq, acc_t[...] * scale)

    top[...] = jnp.full_like(top, LOW)

    def take_b(d, _):
        take_mate(1, 2 * d + 1 - core)
        return 0

    lax.fori_loop(0, chips, take_b, 0)

    def first_b(i, _):
        score_pair(1, i, q_b)
        return 0

    lax.fori_loop(0, chips, first_b, 0)
    peak_b = jnp.max(top[...], axis=0, keepdims=True) * factor
    tot[...] = jnp.zeros_like(tot)
    acc_t[...] = jnp.zeros_like(acc_t)

    def second_b(i, _):
        p = jnp.exp2(scores[i] * factor - peak_b)
        tot[...] += groups(p, jnp.add)
        acc_t[...] += dot_tn(kv[1, pl.ds(2 * i, 2), 1].reshape(2 * tok, dim), p.astype(BF16))
        return 0

    lax.fori_loop(0, chips, second_b, 0)
    total_b = jnp.sum(tot[...], axis=0, keepdims=True)
    put(out_b, acc_t[...] / total_b)

    pair(chip).wait_recv()
    own[chip] = own[chip] + pair_in[chip].astype(F32)

    def gather_sum(off, _):
        d = lax.rem(chip + off, chips)
        pltpu.make_async_remote_copy(
            src_ref=far_out.at[d], dst_ref=far_in.at[d],
            send_sem=far_send.at[d], recv_sem=far_recv.at[d], **to(d * 2 + core),
        ).wait_recv()
        own[chip] = own[chip] + far_in[d].astype(F32)
        return 0

    lax.fori_loop(1, chips, gather_sum, 0)
    out_dk[...] = (own[chip, 0] * scale).astype(BF16)
    out_dv[...] = own[chip, 1].astype(BF16)

    def drain_far(off, _):
        far(lax.rem(chip + off, chips)).wait_send()
        return 0

    lax.fori_loop(1, chips, drain_far, 0)

    def drain(d, _):
        pair(d).wait_send()
        slot = 2 * d + core
        for b in range(2):
            for j in range(2):
                go_mate(b, slot, j).wait_send()

                @pl.when(jnp.logical_and(can_right, d <= chip))
                def _():
                    go_right(b, slot, j).wait_send()

                @pl.when(jnp.logical_and(can_left, d >= chip))
                def _():
                    go_left(b, slot, j).wait_send()
        return 0

    lax.fori_loop(0, chips, drain, 0)


def emit(*refs):
    count = len(refs) // 2
    sems = refs[-1]
    copies = [
        pltpu.make_async_copy(refs[i], refs[count + i], sems.at[i]) for i in range(count)
    ]
    for copy in copies:
        copy.start()
    for copy in copies:
        copy.wait()


def on_device(n, qa, ka, va, ga, qb, kb, vb, owner):
    tok, dim = ka.shape
    heads = qa.shape[1] // dim
    rows = heads * tok
    chips = n // 2
    any_spec = pl.BlockSpec(memory_space=pl.ANY)
    sem = pltpu.SemaphoreType.DMA
    vmem_spec = pl.BlockSpec(memory_space=pltpu.VMEM)
    outs = pl.pallas_call(
        functools.partial(kernel, n, tok, heads, dim),
        out_shape=(
            pltpu.VMEM(qb.shape, BF16),
            pltpu.VMEM(qa.shape, BF16),
            pltpu.VMEM(ka.shape, BF16),
            pltpu.VMEM(va.shape, BF16),
        ),
        in_specs=[pl.BlockSpec(memory_space=pltpu.SMEM)] + [any_spec] * 7,
        out_specs=(vmem_spec,) * 4,
        scratch_shapes=[
            pltpu.VMEM((2, n, 2, tok, dim), BF16),
            pltpu.VMEM((rows, dim), BF16),
            pltpu.VMEM((rows, dim), BF16),
            pltpu.VMEM((rows, dim), BF16),
            pltpu.VMEM((chips, 2 * tok, rows), F32),
            pltpu.VMEM((chips, 2 * tok, rows), F32),
            pltpu.VMEM((8, rows), F32),
            pltpu.VMEM((8, rows), F32),
            pltpu.VMEM((8, rows), F32),
            pltpu.VMEM((dim, rows), F32),
            pltpu.VMEM((2, 2, tok, dim), F32),
            pltpu.VMEM((chips, 2, tok, dim), F32),
            pltpu.VMEM((chips, 2, tok, dim), BF16),
            pltpu.VMEM((chips, 2, tok, dim), BF16),
            pltpu.VMEM((chips, 2, tok, dim), BF16),
            pltpu.VMEM((chips, 2, tok, dim), BF16),
            sem((4 + 3 * heads,)),
            sem((2, n, 2)),
            sem((2, n, 2)),
            sem((2, n, 2)),
            sem((2, n, 2)),
            sem((chips,)),
            sem((chips,)),
            sem((chips,)),
            sem((chips,)),
        ],
        compiler_params=pltpu.CompilerParams(collective_id=0, has_side_effects=True),
    )(owner, qa, ka, va, ga, qb, kb, vb)
    return pl.pallas_call(
        emit,
        out_shape=tuple(jax.ShapeDtypeStruct(x.shape, x.dtype) for x in outs),
        in_specs=[vmem_spec] * 4,
        out_specs=(any_spec,) * 4,
        scratch_shapes=[sem((4,))],
        compiler_params=pltpu.CompilerParams(vmem_limit_bytes=8 * 2**20),
    )(*outs)


def solution(mesh):
    spec = P(("dp", "context"), "tensor")
    return jax.shard_map(
        functools.partial(on_device, mesh.shape["context"]),
        mesh=mesh,
        in_specs=(spec,) * 7 + (P(),),
        out_specs=(spec,) * 4,
        check_vma=False,
    )
```

profile of v0, /device:TPU:0, one launch (start us, length us, event | category | flops | bytes accessed | tf_op | source)
XLA Modules:
  0.0 26.1 jit_solution(4236489964123974483)
XLA Ops:
  0.6 24.7 %shard_map.111 = (bf16[128,512]{1,0:T(8,128)(2,1)S(1)}, bf16[128,512]{1,0:T(8,128)(2,1)S(1)}, bf16[128,128]{1,0:T(8,128)(2,1)S(1)}, bf16[128,128]{1,0:T(8,128)(2,1)S(1)}) custom-call(s32[8]{0:T(128)} %owner.1, bf16[128,512]{1,0:T(8,128)(2,1)} %qa.1, bf16[128,128]{1,0:T(8,128)(2,1)} %ka.1, bf16[128,128]{1,0:T(8,128)(2,1)} %va.1, bf16[128,512]{1,0:T(8,128)(2,1)} %ga.1, ...), custom_call_target="tpu_custom_call" | custom-call | tf_op jit(solution)/shard_map/pallas_call | solution.py:353
  25.4 0.7 %shard_map.112 = (bf16[128,512]{1,0:T(8,128)(2,1)}, bf16[128,512]{1,0:T(8,128)(2,1)}, bf16[128,128]{1,0:T(8,128)(2,1)}, bf16[128,128]{1,0:T(8,128)(2,1)}) custom-call(bf16[128,512]{1,0:T(8,128)(2,1)S(1)} %get-tuple-element.8.refs_0_, bf16[128,512]{1,0:T(8,128)(2,1)S(1)} %get-tuple-element.9.refs_1_, bf16[128,128]{1,0:T(8,128)(2,1)S(1)} %get-tuple-element.10.refs_2_, ...), custom_call_target="tpu_custom_call" | custom-call | tf_op jit(solution)/shard_map/pallas_call | solution.py:392
where the time goes:
time: 26.3 us; the launch traced here: 26.1 us
  Pallas kernels  25.5 us (97%)
  between operations  0.64 us (2%)
    pallas_call x1, Pallas kernels, on_device(): pl.pallas_call(functools.partial(kernel, n, tok, heads, dim), out_shape=(...  24.7 us
    pallas_call x1, Pallas kernels, on_device(): pl.pallas_call(emit, out_shape=tuple((jax.ShapeDtypeStruct(x.shape, x.dty...  0.75 us

commit v1 on v0

v1 whole, which is shorter than its diff:
```python
import functools

import jax
import jax.numpy as jnp
from jax import lax
from jax.experimental import pallas as pl
from jax.experimental.pallas import tpu as pltpu
from jax.sharding import PartitionSpec as P

LOW = -1e30
LOG2E = 1.4426950408889634
F32 = jnp.float32
BF16 = jnp.bfloat16


def dot_nt(a, b):
    return lax.dot_general(a, b, (((1,), (1,)), ((), ())), preferred_element_type=F32)


def dot_nn(a, b):
    return lax.dot_general(a, b, (((1,), (0,)), ((), ())), preferred_element_type=F32)


def dot_tn(a, b):
    return lax.dot_general(a, b, (((0,), (0,)), ((), ())), preferred_element_type=F32)


def each(lo, hi, body):
    if hi - lo <= 4:
        for t in range(lo, hi):
            body(t)
    else:
        lax.fori_loop(lo, hi, lambda t, _: (body(t), 0)[1], 0)


def kernel(
    n, tok, heads, dim,
    owner_in, qa, ka, va, ga, qb, kb, vb,
    out_b, out_dq, out_dk, out_dv,
    owner, kv, qa0, ga0, qb0, qa1, ga1, qb1,
    e_a, e_b, pg, m_a, t_a, d_a, m_b, t_b,
    st_out, st_in, glob, sb_out, sb_in,
    sg_hi, sg_lo, p_hi, p_lo, dq_own, dq_out, dq_in, ob_own, ob_out, ob_in,
    gf, gs, rp, ms, rf,
    load_sem, kv_recv, g_send, f_send, mate_send, mate_recv,
    p_send, p_recv, x_send, x_recv,
):
    chips = n // 2
    pairs = chips // 2
    half = tok // 2
    rows = heads * half
    me = lax.axis_index("context")
    chip, core = me // 2, me % 2
    mate = chip * 2 + (1 - core)
    pair, side = chip // 2, chip % 2
    partner = pair * 2 + (1 - side)
    factor = dim ** (-0.5) * LOG2E
    scale = dim ** (-0.5)
    extra = 4 * chips

    def remote(src, dst, send, recv, idx):
        return pltpu.make_async_remote_copy(
            src_ref=src, dst_ref=dst, send_sem=send, recv_sem=recv,
            device_id={"context": idx}, device_id_type=pl.DeviceIdType.MESH,
        )

    def chip_at(t):
        other = lax.rem(pair + t // 2, pairs)
        right = (other > pair).astype(jnp.int32)
        far = t % 2
        away = other * 2 + jnp.where(far == 1, right, 1 - right)
        return jnp.where(t == 0, chip, jnp.where(t == 1, partner, away))

    def is_near(d):
        return jnp.where(d > chip, side == 1, side == 0)

    def outside(d):
        return d // 2 != pair

    def kv_load(b, j):
        src = ((ka, va), (kb, vb))[b][j]
        return pltpu.make_async_copy(src, kv.at[b, j, chip], load_sem.at[b * 2 + j])

    own_rows = (qa0, ga0, qb0)
    mate_rows = (qa1, ga1, qb1)

    def row_load(i, part, h):
        src = (qa, ga, qb)[i]
        return pltpu.make_async_copy(
            src.at[pl.ds(part * half, half), pl.ds(h * dim, dim)],
            own_rows[i].at[part, pl.ds(h * half, half), :],
            load_sem.at[5 + (i * 2 + part) * heads + h],
        )

    owner_load = pltpu.make_async_copy(owner_in, owner, load_sem.at[4])

    for j in range(2):
        kv_load(0, j).start()
    owner_load.start()
    for part in range(2):
        for h in range(heads):
            row_load(0, part, h).start()
    for j in range(2):
        kv_load(1, j).start()
    for i in (1, 2):
        for part in range(2):
            for h in range(heads):
                row_load(i, part, h).start()

    barrier = pltpu.get_barrier_semaphore()
    pl.semaphore_signal(
        barrier, inc=1, device_id={"context": mate}, device_id_type=pl.DeviceIdType.MESH
    )
    count = jnp.int32(1)
    for off in range(1, chips):
        d = lax.rem(chip + off, chips)
        low, high = jnp.minimum(chip, d), jnp.maximum(chip, d)
        meet = jnp.logical_or(
            jnp.logical_not(outside(d)), jnp.logical_or(low % 2 == 1, high % 2 == 0)
        )
        count = count + meet.astype(jnp.int32)

        @pl.when(meet)
        def _():
            pl.semaphore_signal(
                barrier, inc=1, device_id={"context": d * 2 + core},
                device_id_type=pl.DeviceIdType.MESH,
            )

    def give(b, j, target):
        return remote(
            kv.at[b, j, chip], kv.at[b, j, chip], g_send.at[b, j, target],
            kv_recv.at[b, j, chip], target * 2 + core,
        )

    def nearest(k):
        other = lax.rem(pair + k, pairs)
        return other * 2 + (other < pair).astype(jnp.int32)

    def give_all(b, j):
        each(1, pairs, lambda k: give(b, j, nearest(k)).start())
        give(b, j, partner).start()

    def forward(b, j, d):
        return remote(
            kv.at[b, j, d], kv.at[b, j, d], f_send.at[b, j, d],
            kv_recv.at[b, j, d], partner * 2 + core,
        )

    def take(b, j, d):
        forward(b, j, d).wait_recv()

    def pass_on(b, j, d):
        @pl.when(jnp.logical_and(outside(d), is_near(d)))
        def _():
            forward(b, j, d).start()

    def to_mate(k):
        src, dst = (
            (qa0, qa1), (ga0, ga1), (qb0, qb1), (st_out, st_in),
            (dq_out, dq_in), (ob_out, ob_in), (sb_out, sb_in),
        )[k]
        return remote(src, dst, mate_send.at[k], mate_recv.at[k], mate)

    kv_load(0, 0).wait()
    pl.semaphore_wait(barrier, count)
    give_all(0, 0)
    kv_load(0, 1).wait()
    give_all(0, 1)

    def rows_ready(i):
        for part in range(2):
            for h in range(heads):
                row_load(i, part, h).wait()
        to_mate(i).start()

    rows_ready(0)
    for j in range(2):
        kv_load(1, j).wait()
    for j in range(2):
        give_all(1, j)
    rows_ready(1)
    rows_ready(2)
    owner_load.wait()

    mine = (owner[me], owner[mate])

    def later(q, d):
        return (owner[2 * d + core] > mine[q]).astype(jnp.int32)

    lane = lax.broadcasted_iota(jnp.int32, (half, rows), 1) % half
    kept = lax.broadcasted_iota(jnp.int32, (half, rows), 0) <= lane

    def finish(e, m, tot, i, raw):
        top = jnp.max(raw, axis=0, keepdims=True)
        x = jnp.exp2(raw * factor - top * factor)
        e[i] = x
        m[i] = top
        tot[i] = jnp.sum(x, axis=0, keepdims=True)

    def pick(q, d, block):
        return jnp.where(later(q, d) == 1, block[half:], block[:half])

    def score_own(b, e, m, tot, queries):
        keys = kv[b, 0, chip]
        high = dot_nt(keys, queries[1])
        low = dot_nt(keys[:half], queries[0])
        finish(e, m, tot, 4 * chip, high[:half])
        finish(e, m, tot, 4 * chip + 1, jnp.where(kept, low, LOW))
        finish(e, m, tot, extra, jnp.where(kept, high[half:], LOW))

    def score(b, e, m, tot, q, d, queries):
        keys = kv[b, 0, d]
        finish(e, m, tot, 4 * d + 2 * q, dot_nt(keys[:half], queries[1]))
        finish(e, m, tot, 4 * d + 2 * q + 1, dot_nt(pick(q, d, keys), queries[later(q, d)]))

    def slope(i, x):
        pg[i] = x
        d_a[i] = jnp.sum(e_a[i] * x, axis=0, keepdims=True)

    def slope_own(grads):
        values = kv[0, 1, chip]
        high = dot_nt(values, grads[1])
        slope(4 * chip, high[:half])
        slope(4 * chip + 1, dot_nt(values[:half], grads[0]))
        slope(extra, high[half:])

    def slopes(q, d, grads):
        values = kv[0, 1, d]
        slope(4 * d + 2 * q, dot_nt(values[:half], grads[1]))
        slope(4 * d + 2 * q + 1, dot_nt(pick(q, d, values), grads[later(q, d)]))

    score_own(0, e_a, m_a, t_a, qa0)
    slope_own(ga0)
    to_mate(0).wait_recv()
    score(0, e_a, m_a, t_a, 1, chip, qa1)
    to_mate(1).wait_recv()
    slopes(1, chip, ga1)

    def keys_a(t):
        d = chip_at(t)
        take(0, 0, d)
        pass_on(0, 0, d)
        score(0, e_a, m_a, t_a, 0, d, qa0)
        score(0, e_a, m_a, t_a, 1, d, qa1)

    each(1, chips, keys_a)

    def values_a(t):
        d = chip_at(t)
        take(0, 1, d)
        pass_on(0, 1, d)
        slopes(0, d, ga0)
        slopes(1, d, ga1)

    each(1, chips, values_a)

    def combine(m, sums, out):
        for q in range(2):
            tops = [jnp.full((1, rows), LOW, F32) for _ in range(2)]
            for d in range(chips):
                i = 4 * d + 2 * q
                up = later(q, d) == 1
                tops[1] = jnp.maximum(tops[1], jnp.maximum(m[i], jnp.where(up, m[i + 1], LOW)))
                tops[0] = jnp.maximum(tops[0], jnp.where(up, LOW, m[i + 1]))
            if q == 0:
                tops[1] = jnp.maximum(tops[1], m[extra])
            acc = [[jnp.zeros((1, rows), F32) for _ in range(2)] for _ in sums]
            for d in range(chips):
                i = 4 * d + 2 * q
                up = later(q, d) == 1
                w1 = jnp.exp2((m[i] - tops[1]) * factor)
                w2 = jnp.exp2((m[i + 1] - jnp.where(up, tops[1], tops[0])) * factor)
                for a, s in zip(acc, sums):
                    second = s[i + 1] * w2
                    a[1] = a[1] + s[i] * w1 + jnp.where(up, second, 0.0)
                    a[0] = a[0] + jnp.where(up, 0.0, second)
            if q == 0:
                w1 = jnp.exp2((m[extra] - tops[1]) * factor)
                for a, s in zip(acc, sums):
                    a[1] = a[1] + s[extra] * w1
            for part in range(2):
                r = 2 * q + part
                out[r:r + 1] = tops[part]
                for k, a in enumerate(acc):
                    r = 4 * (k + 1) + 2 * q + part
                    out[r:r + 1] = a[part]

    combine(m_a, (t_a, d_a), st_out)
    to_mate(3).start()

    def relay_b(t):
        d = chip_at(t)

        @pl.when(is_near(d))
        def _():
            for j in range(2):
                take(1, j, d)
                forward(1, j, d).start()

    each(2, chips, relay_b)

    to_mate(3).wait_recv()
    for q in range(2):
        for part in range(2):
            r, s = 2 * q + part, 2 * (1 - q) + part
            m1, m2 = st_out[r:r + 1], st_in[s:s + 1]
            top = jnp.maximum(m1, m2)
            c1, c2 = jnp.exp2((m1 - top) * factor), jnp.exp2((m2 - top) * factor)
            inv = 1.0 / (st_out[4 + r:5 + r] * c1 + st_in[4 + s:5 + s] * c2)
            glob[r:r + 1] = top
            glob[4 + r:5 + r] = inv
            glob[8 + r:9 + r] = (st_out[8 + r:9 + r] * c1 + st_in[8 + s:9 + s] * c2) * inv

    def grad_item(i, stats):
        top, inv, delta = stats
        p = e_a[i] * (jnp.exp2((m_a[i] - top) * factor) * inv)
        return p.astype(BF16), (p * (pg[i] - delta)).astype(BF16)

    def stats_of(q, part):
        r = 2 * q + part
        return glob[r:r + 1], glob[4 + r:5 + r], glob[8 + r:9 + r]

    zero = jnp.zeros((half, rows), BF16)

    def grads(d, own):
        low, high = [0.0, 0.0], [0.0, 0.0]
        for q in range(2):
            side_rows = ((ga0, qa0), (ga1, qa1))[q]
            upper, lower = stats_of(q, 1), stats_of(q, 0)
            first = grad_item(4 * d + 2 * q, upper)
            sg_hi[q, d, 0:half] = first[1]
            if own and q == 0:
                second = grad_item(4 * d + 1, lower)
                third = grad_item(extra, upper)
                sg_hi[q, d, half:tok] = third[1]
                sg_lo[q, d] = second[1]
                for k in range(2):
                    low[k] += dot_nn(first[k], side_rows[k][1]) + dot_nn(second[k], side_rows[k][0])
                    high[k] += dot_nn(third[k], side_rows[k][1])
            else:
                at = later(q, d)
                up = at == 1
                second = grad_item(
                    4 * d + 2 * q + 1, [jnp.where(up, x, y) for x, y in zip(upper, lower)]
                )
                sg_hi[q, d, half:tok] = jnp.where(up, second[1], zero)
                sg_lo[q, d] = jnp.where(up, zero, second[1])
                for k in range(2):
                    r = dot_nn(second[k], side_rows[k][at])
                    low[k] += dot_nn(first[k], side_rows[k][1]) + jnp.where(up, 0.0, r)
                    high[k] += jnp.where(up, r, 0.0)
        return low, high

    def to_partner(k, d):
        return remote(
            gs.at[k, d], rp.at[k, d], p_send.at[k, d], p_recv.at[k, d], partner * 2 + core
        )

    def to_owner(k, d):
        return remote(
            ms.at[k, d], rf.at[k, pair], x_send.at[k, d], x_recv.at[k, pair], d * 2 + core
        )

    def merges(d):
        return jnp.logical_and(outside(d), is_near(d))

    def grads_away(u):
        d = chip_at(chips - 1 - u)
        low, high = grads(d, False)
        for k in range(2):
            gs[k, d, 0:half] = low[k].astype(BF16)
            gs[k, d, half:tok] = high[k].astype(BF16)
            gf[k, d, 0:half] = low[k]
            gf[k, d, half:tok] = high[k]

        @pl.when(jnp.logical_not(merges(d)))
        def _():
            for k in range(2):
                to_partner(k, d).start()

    each(0, chips - 1, grads_away)
    low, high = grads(chip, True)
    for k in range(2):
        gf[k, chip, 0:half] = low[k]
        gf[k, chip, half:tok] = high[k]

    def spread(hi, lo, left, q, out):
        out[1] = dot_tn(left.reshape(chips * tok, dim), hi[q].reshape(chips * tok, rows))
        out[0] = dot_tn(
            left[:, :half].reshape(chips * half, dim), lo[q].reshape(chips * half, rows)
        )

    keys_all = kv[0, 0]
    spread(sg_hi, sg_lo, keys_all, 1, dq_out)
    to_mate(4).start()
    spread(sg_hi, sg_lo, keys_all, 0, dq_own)

    score_own(1, e_b, m_b, t_b, qb0)
    to_mate(2).wait_recv()
    score(1, e_b, m_b, t_b, 1, chip, qb1)

    def keys_b(t):
        d = chip_at(t)

        @pl.when(jnp.logical_not(merges(d)))
        def _():
            for j in range(2):
                take(1, j, d)
        score(1, e_b, m_b, t_b, 0, d, qb0)
        score(1, e_b, m_b, t_b, 1, d, qb1)

    each(1, chips, keys_b)

    def merge(u):
        d = chip_at(chips - 1 - u)

        @pl.when(merges(d))
        def _():
            for k in range(2):
                to_partner(k, d).wait_recv()
                ms[k, d] = (gf[k, d] + rp[k, d].astype(F32)).astype(BF16)
                to_owner(k, d).start()

    each(0, chips - 2, merge)

    combine(m_b, (t_b,), sb_out)
    to_mate(6).start()

    def weigh(d):
        for q in range(2):
            i = 4 * d + 2 * q
            up = later(q, d) == 1
            lower, upper = (sb_out[2 * q + part:2 * q + part + 1] for part in range(2))
            w1 = jnp.exp2((m_b[i] - upper) * factor)
            w2 = jnp.exp2((m_b[i + 1] - jnp.where(up, upper, lower)) * factor)
            second = (e_b[i + 1] * w2).astype(BF16)
            p_hi[q, d, 0:half] = (e_b[i] * w1).astype(BF16)
            p_hi[q, d, half:tok] = jnp.where(up, second, zero)
            p_lo[q, d] = jnp.where(up, zero, second)

    each(0, chips, weigh)
    w = jnp.exp2((m_b[extra] - sb_out[1:2]) * factor)
    p_hi[0, chip, half:tok] = (e_b[extra] * w).astype(BF16)

    values_all = kv[1, 1]
    spread(p_hi, p_lo, values_all, 1, ob_out)
    to_mate(5).start()
    spread(p_hi, p_lo, values_all, 0, ob_own)

    def put(out, part, x):
        low = jnp.transpose(x).astype(BF16)
        for h in range(heads):
            out[part * half:(part + 1) * half, h * dim:(h + 1) * dim] = (
                low[h * half:(h + 1) * half]
            )

    to_mate(4).wait_recv()
    for part in range(2):
        put(out_dq, part, (dq_own[part] + dq_in[part]) * scale)

    to_mate(6).wait_recv()
    to_mate(5).wait_recv()
    for part in range(2):
        m1, m2 = sb_out[part:part + 1], sb_in[2 + part:3 + part]
        top = jnp.maximum(m1, m2)
        c1, c2 = jnp.exp2((m1 - top) * factor), jnp.exp2((m2 - top) * factor)
        inv = 1.0 / (sb_out[4 + part:5 + part] * c1 + sb_in[6 + part:7 + part] * c2)
        put(out_b, part, ob_own[part] * (c1 * inv) + ob_in[part] * (c2 * inv))

    for k in range(2):
        to_partner(k, chip).wait_recv()
        gf[k, chip] = gf[k, chip] + rp[k, chip].astype(F32)

    def add_far(u):
        other = lax.rem(pair + u, pairs)
        for k in range(2):
            remote(
                ms.at[k, chip], rf.at[k, other], x_send.at[k, chip], x_recv.at[k, other], mate
            ).wait_recv()
            gf[k, chip] = gf[k, chip] + rf[k, other].astype(F32)

    each(1, pairs, add_far)
    out_dv[...] = gf[0, chip].astype(BF16)
    out_dk[...] = (gf[1, chip] * scale).astype(BF16)

    for k in range(7):
        to_mate(k).wait_send()
    for b in range(2):
        for j in range(2):
            each(1, pairs, lambda k: give(b, j, nearest(k)).wait_send())
            give(b, j, partner).wait_send()

    def drain(t):
        d = chip_at(t)
        near = merges(d)

        @pl.when(near)
        def _():
            for b in range(2):
                for j in range(2):
                    forward(b, j, d).wait_send()
            for k in range(2):
                to_owner(k, d).wait_send()

        @pl.when(jnp.logical_not(near))
        def _():
            for k in range(2):
                to_partner(k, d).wait_send()

    each(1, chips, drain)


def emit(*refs):
    count = len(refs) // 2
    sems = refs[-1]
    copies = [
        pltpu.make_async_copy(refs[i], refs[count + i], sems.at[i]) for i in range(count)
    ]
    for copy in copies:
        copy.start()
    for copy in copies:
        copy.wait()


def on_device(n, qa, ka, va, ga, qb, kb, vb, owner):
    tok, dim = ka.shape
    heads = qa.shape[1] // dim
    chips = n // 2
    pairs = chips // 2
    half = tok // 2
    rows = heads * half
    items = 4 * chips + 1
    any_spec = pl.BlockSpec(memory_space=pl.ANY)
    vmem_spec = pl.BlockSpec(memory_space=pltpu.VMEM)
    dma = pltpu.SemaphoreType.DMA
    vmem = pltpu.VMEM
    queries = vmem((2, rows, dim), BF16)
    block = vmem((items, half, rows), F32)
    line = vmem((items, 1, rows), F32)
    stats = vmem((16, rows), F32)
    high = vmem((2, chips, tok, rows), BF16)
    low = vmem((2, chips, half, rows), BF16)
    turned = vmem((2, dim, rows), F32)
    outs = pl.pallas_call(
        functools.partial(kernel, n, tok, heads, dim),
        out_shape=(
            pltpu.VMEM(qb.shape, BF16),
            pltpu.VMEM(qa.shape, BF16),
            pltpu.VMEM(ka.shape, BF16),
            pltpu.VMEM(va.shape, BF16),
        ),
        in_specs=[any_spec] * 8,
        out_specs=(vmem_spec,) * 4,
        scratch_shapes=[
            pltpu.SMEM(owner.shape, jnp.int32),
            vmem((2, 2, chips, tok, dim), BF16),
            queries, queries, queries, queries, queries, queries,
            block, block, block,
            line, line, line, line, line,
            stats, stats, stats, stats, stats,
            high, low, high, low,
            turned, turned, turned, turned, turned, turned,
            vmem((2, chips, tok, dim), F32),
            vmem((2, chips, tok, dim), BF16),
            vmem((2, chips, tok, dim), BF16),
            vmem((2, chips, tok, dim), BF16),
            vmem((2, pairs, tok, dim), BF16),
            dma((5 + 6 * heads,)),
            dma((2, 2, chips)),
            dma((2, 2, chips)),
            dma((2, 2, chips)),
            dma((7,)),
            dma((7,)),
            dma((2, chips)),
            dma((2, chips)),
            dma((2, chips)),
            dma((2, pairs)),
        ],
        compiler_params=pltpu.CompilerParams(collective_id=0, has_side_effects=True),
    )(owner, qa, ka, va, ga, qb, kb, vb)
    return pl.pallas_call(
        emit,
        out_shape=tuple(jax.ShapeDtypeStruct(x.shape, x.dtype) for x in outs),
        in_specs=[vmem_spec] * 4,
        out_specs=(any_spec,) * 4,
        scratch_shapes=[dma((4,))],
        compiler_params=pltpu.CompilerParams(vmem_limit_bytes=8 * 2**20),
    )(*outs)


def solution(mesh):
    spec = P(("dp", "context"), "tensor")
    return jax.shard_map(
        functools.partial(on_device, mesh.shape["context"]),
        mesh=mesh,
        in_specs=(spec,) * 7 + (P(),),
        out_specs=(spec,) * 4,
        check_vma=False,
    )
```

time: 26.3 us -> 24.2 us (0.920)
  Pallas kernels: 25.5 us -> 23.4 us
    pallas_call x1, Pallas kernels: 24.7 us -> 22.6 us  [on_device(): pl.pallas_call(functools.partial(kernel, n, tok, heads, dim), out_shape=(...]
where the time goes in v1:
time: 24.2 us; the launch traced here: 24 us
  Pallas kernels  23.4 us (97%)
  between operations  0.64 us (3%)
    pallas_call x1, Pallas kernels, on_device(): pl.pallas_call(functools.partial(kernel, n, tok, heads, dim), out_shape=(...  22.6 us
    pallas_call x1, Pallas kernels, on_device(): pl.pallas_call(emit, out_shape=tuple((jax.ShapeDtypeStruct(x.shape, x.dty...  0.75 us

profile of v1, /device:TPU:0, one launch (start us, length us, event | category | flops | bytes accessed | tf_op | source)
XLA Modules:
  0.0 24.0 jit_solution(173329161359963601)
XLA Ops:
  0.6 22.6 %shard_map.111 = (bf16[128,512]{1,0:T(8,128)(2,1)S(1)}, bf16[128,512]{1,0:T(8,128)(2,1)S(1)}, bf16[128,128]{1,0:T(8,128)(2,1)S(1)}, bf16[128,128]{1,0:T(8,128)(2,1)S(1)}) custom-call(s32[8]{0:T(128)} %owner_in.1, bf16[128,512]{1,0:T(8,128)(2,1)} %qa.1, bf16[128,128]{1,0:T(8,128)(2,1)} %ka.1, bf16[128,128]{1,0:T(8,128)(2,1)} %va.1, bf16[128,512]{1,0:T(8,128)(2,1)} %ga.1, ...), custom_call_target="tpu_custom_call" | custom-call | tf_op jit(solution)/shard_map/pallas_call | solution.py:545
  23.3 0.7 %shard_map.112 = (bf16[128,512]{1,0:T(8,128)(2,1)}, bf16[128,512]{1,0:T(8,128)(2,1)}, bf16[128,128]{1,0:T(8,128)(2,1)}, bf16[128,128]{1,0:T(8,128)(2,1)}) custom-call(bf16[128,512]{1,0:T(8,128)(2,1)S(1)} %get-tuple-element.8.refs_0_, bf16[128,512]{1,0:T(8,128)(2,1)S(1)} %get-tuple-element.9.refs_1_, bf16[128,128]{1,0:T(8,128)(2,1)S(1)} %get-tuple-element.10.refs_2_, ...), custom_call_target="tpu_custom_call" | custom-call | tf_op jit(solution)/shard_map/pallas_call | solution.py:582
